TPU v7x, 128 devices: a whole 4x4x4 slice. The times are simulated.
128 devices in a mesh: cell: 8 (over z_hi, y), idx: 16 (over z_lo, x, core).
Axes of the slice: x: 4, y: 4, z: 4 (z_hi: 2, z_lo: 2; z = z_hi * 2 + z_lo), core: 2. Of those that a mesh axis runs over, the one named last changes fastest.
Arguments:
- coeffs: bfloat16 [12288, 2048], P('cell', 'idx'), may hold values from -6 to 6
- tensor: bfloat16 [16, 2048, 2048], P('cell', 'idx'), may hold values from -0.0029296875 to 0.0029296875
Outputs:
- collision: float32 [16, 12288], P(None, ('cell', 'idx'))
All inputs are finite; a program needn't handle non-finite values.
Results may differ from a plain program's by a relative error of at most 0.0003.
Values may be sent and summed in bfloat16 or wider, within the bound.
A program may use at most 64 MiB of HBM per device.

v0:
```python
import jax
import jax.numpy as jnp
from jax import lax
from jax.sharding import PartitionSpec as P


def passed_along(shard, axis, by):
    devices = lax.axis_size(axis)
    return lax.ppermute(shard, axis, [(i, (i + by) % devices) for i in range(devices)])


def split_up(shard, dim, devices):
    shape = shard.shape
    tiles = shard.reshape(*shape[:dim], devices, shape[dim] // devices, *shape[dim + 1 :])
    return jnp.moveaxis(tiles, dim, 0)


def sum_at_owner(shard, axis, dim):
    devices = lax.axis_size(axis)
    tiles = lax.all_to_all(split_up(shard, dim, devices), axis, 0, 0, tiled=True)
    return jnp.sum(tiles, axis=0)


def contract(slab, rows, whole):
    outputs, inner, width = slab.shape
    mixed = lax.dot_general(
        slab.reshape(outputs * inner, width),
        whole,
        (((1,), (1,)), ((), ())),
        preferred_element_type=jnp.float32,
    )
    mixed = mixed.reshape(outputs, inner, whole.shape[0])
    return jnp.sum(mixed * jnp.transpose(rows).astype(jnp.float32)[None], axis=1)


def shards(coeffs, tensor):
    whole = lax.all_gather(coeffs, "idx", axis=1, tiled=True)
    ncell = lax.axis_size("cell")
    myself = lax.axis_index("cell")
    outputs, inner, width = tensor.shape
    cells = whole.shape[0]
    start_acc = jnp.zeros((outputs * ncell, cells), jnp.float32)

    def deposit(acc, contribs, owners):
        stacked = jnp.concatenate(contribs, axis=0)
        for number, owner in enumerate(owners):
            piece = stacked[number * outputs : (number + 1) * outputs]
            place = owner * outputs
            current = lax.dynamic_slice(acc, (place, jnp.int32(0)), (outputs, cells))
            acc = lax.dynamic_update_slice(acc, current + piece, (place, jnp.int32(0)))
        return acc

    half = inner // 2
    rows_upper = coeffs[:, :half]
    rows_lower = coeffs[:, half:]

    def turn_double(step, carry):
        upper, lower, acc = carry
        acc = deposit(
            acc,
            [contract(upper, rows_upper, whole), contract(lower, rows_lower, whole)],
            [(myself - step) % ncell, (myself + step) % ncell],
        )
        upper = passed_along(upper, "cell", 1)
        lower = passed_along(lower, "cell", -1)
        return (upper, lower, acc)

    upper, lower, acc = lax.fori_loop(
        0, ncell - 1, turn_double, (tensor[:, :half], tensor[:, half:], start_acc)
    )
    final = ncell - 1
    acc = deposit(
        acc,
        [contract(upper, rows_upper, whole), contract(lower, rows_lower, whole)],
        [(myself - final) % ncell, (myself + final) % ncell],
    )
    return sum_at_owner(acc, "idx", 1)


def solution(mesh):
    return jax.shard_map(
        shards,
        mesh=mesh,
        in_specs=(P("cell", "idx"), P("cell", "idx", None)),
        out_specs=P(None, ("cell", "idx")),
        check_vma=False,
    )
```

profile of v0, /device:TPU:1, one launch (start us, length us, event | category | flops | bytes accessed | tf_op | source)
XLA Modules:
  0.0 225.6 jit_solution(18109419294492547072)
XLA Ops:
  6.5 0.7 all-gather.2.cloned.1.call-update
  7.3 1.3 fusion.33
  8.6 0.2 copy.10
  8.9 0.8 convert_bitcast_fusion.3
  9.7 0.8 convert_bitcast_fusion.2
  10.5 2.3 %fusion.32 = (bf16[2,64,2048]{2,1,0:T(8,128)(2,1)}, bf16[2,64,2048]{2,1,0:T(8,128)(2,1)}) fusion(bf16[2,128,2048]{2,1,0:T(8,128)(2,1)} %param.5), kind=kLoop, calls=%fused_computation.24 | loop fusion | bytes 2097152 | tf_op jit(solution)/shard_map/slice | solution.py:69
  12.8 52.5 %all-gather.2.cloned.1.call-done = bf16[1536,2048]{1,0:T(8,128)(2,1)} async-done(((bf16[1536,128]{1,0:T(8,128)(2,1)}), bf16[1536,2048]{1,0:T(8,128)(2,1)}) %all-gather.2.cloned.1.call-update) | async-done | bytes 6291472 | tf_op jit(solution)/shard_map/all_gather | solution.py:37
  65.2 0.6 broadcast_in_dim.11
  65.9 128.1 %while.19 = (s32[]{:T(128)}, bf16[2,64,2048]{2,1,0:T(8,128)(2,1)}, bf16[2,64,2048]{2,1,0:T(8,128)(2,1)}, f32[16,1536]{1,0:T(8,128)}, s32[]{:T(128)}, /*index=5*/...) while((s32[]{:T(128)}, bf16[2,64,2048]{2,1,0:T(8,128)(2,1)}, ...), condition=%wide.region_3.4_spmd, body=%wide.region_0.3_spmd.sunk | while | flops 1611595776 | bytes 40862300 | solution.py:68
  65.9 1.0 copy.19
  66.9 1.3 collective-permute-start
  68.2 1.2 copy.20
  69.4 3.8 %collective-permute-start.1 = (bf16[2,64,2048]{2,1,0:T(8,128)(2,1)S(1)}, bf16[2,64,2048]{2,1,0:T(8,128)(2,1)}, u32[]{:S(2)}, u32[]{:S(2)}) collective-permute-start(bf16[2,64,2048]{2,1,0:T(8,128)(2,1)S(1)} %copy.20), channel_id=1, source_target_pairs={{0,112},{16,0},{32,16},{48,32},{64,48},{80,64},{96,80},{112,96},{1... | collective-permute-start | bytes 1572872 | tf_op jit(solution)/shard_map/while/body/eval_jaxpr/ppermute | solution.py:9
  73.3 5.7 %fusion.48 = f32[2,1536]{1,0:T(2,128)} fusion(bf16[2,64,2048]{2,1,0:T(8,128)(2,1)S(1)} %copy.19, bf16[1536,2048]{1,0:T(8,128)(2,1)} %get-tuple-element.317, f32[64,1536]{1,0:T(8,128)S(1)} %get-tuple-element.282), kind=kOutput, calls=%fused_computation.7.clone.1 | convolution fusion | flops 805696512 | bytes 7221248 | tf_op jit(solution)/shard_map/while/body/eval_jaxpr/dot_general | solution.py:26
  79.1 2.2 fusion.49
  81.3 1.4 add_dynamic-update-slice_fusion.6
  82.7 1.4 add_dynamic-update-slice_fusion.7
  84.1 1.0 copy.19
  85.1 1.2 copy.20
  86.3 5.8 %collective-permute-start.1 = (bf16[2,64,2048]{2,1,0:T(8,128)(2,1)S(1)}, bf16[2,64,2048]{2,1,0:T(8,128)(2,1)}, u32[]{:S(2)}, u32[]{:S(2)}) collective-permute-start(bf16[2,64,2048]{2,1,0:T(8,128)(2,1)S(1)} %copy.20), channel_id=1, source_target_pairs={{0,112},{16,0},{32,16},{48,32},{64,48},{80,64},{96,80},{112,96},{1... | collective-permute-start | bytes 1572872 | tf_op jit(solution)/shard_map/while/body/eval_jaxpr/ppermute | solution.py:9
  92.2 5.7 %fusion.48 = f32[2,1536]{1,0:T(2,128)} fusion(bf16[2,64,2048]{2,1,0:T(8,128)(2,1)S(1)} %copy.19, bf16[1536,2048]{1,0:T(8,128)(2,1)} %get-tuple-element.317, f32[64,1536]{1,0:T(8,128)S(1)} %get-tuple-element.282), kind=kOutput, calls=%fused_computation.7.clone.1 | convolution fusion | flops 805696512 | bytes 7221248 | tf_op jit(solution)/shard_map/while/body/eval_jaxpr/dot_general | solution.py:26
  98.0 2.2 fusion.49
  100.2 1.4 add_dynamic-update-slice_fusion.6
  101.6 1.4 add_dynamic-update-slice_fusion.7
  103.0 1.0 copy.19
  104.1 0.9 collective-permute-start
  105.0 1.2 copy.20
  106.1 4.2 %collective-permute-start.1 = (bf16[2,64,2048]{2,1,0:T(8,128)(2,1)S(1)}, bf16[2,64,2048]{2,1,0:T(8,128)(2,1)}, u32[]{:S(2)}, u32[]{:S(2)}) collective-permute-start(bf16[2,64,2048]{2,1,0:T(8,128)(2,1)S(1)} %copy.20), channel_id=1, source_target_pairs={{0,112},{16,0},{32,16},{48,32},{64,48},{80,64},{96,80},{112,96},{1... | collective-permute-start | bytes 1572872 | tf_op jit(solution)/shard_map/while/body/eval_jaxpr/ppermute | solution.py:9
  110.4 5.7 %fusion.48 = f32[2,1536]{1,0:T(2,128)} fusion(bf16[2,64,2048]{2,1,0:T(8,128)(2,1)S(1)} %copy.19, bf16[1536,2048]{1,0:T(8,128)(2,1)} %get-tuple-element.317, f32[64,1536]{1,0:T(8,128)S(1)} %get-tuple-element.282), kind=kOutput, calls=%fused_computation.7.clone.1 | convolution fusion | flops 805696512 | bytes 7221248 | tf_op jit(solution)/shard_map/while/body/eval_jaxpr/dot_general | solution.py:26
  116.2 2.2 fusion.49
  118.4 1.4 add_dynamic-update-slice_fusion.6
  119.8 1.4 add_dynamic-update-slice_fusion.7
  121.2 1.0 copy.19
  122.3 1.2 copy.20
  123.5 5.1 %collective-permute-start.1 = (bf16[2,64,2048]{2,1,0:T(8,128)(2,1)S(1)}, bf16[2,64,2048]{2,1,0:T(8,128)(2,1)}, u32[]{:S(2)}, u32[]{:S(2)}) collective-permute-start(bf16[2,64,2048]{2,1,0:T(8,128)(2,1)S(1)} %copy.20), channel_id=1, source_target_pairs={{0,112},{16,0},{32,16},{48,32},{64,48},{80,64},{96,80},{112,96},{1... | collective-permute-start | bytes 1572872 | tf_op jit(solution)/shard_map/while/body/eval_jaxpr/ppermute | solution.py:9
  128.6 5.7 %fusion.48 = f32[2,1536]{1,0:T(2,128)} fusion(bf16[2,64,2048]{2,1,0:T(8,128)(2,1)S(1)} %copy.19, bf16[1536,2048]{1,0:T(8,128)(2,1)} %get-tuple-element.317, f32[64,1536]{1,0:T(8,128)S(1)} %get-tuple-element.282), kind=kOutput, calls=%fused_computation.7.clone.1 | convolution fusion | flops 805696512 | bytes 7221248 | tf_op jit(solution)/shard_map/while/body/eval_jaxpr/dot_general | solution.py:26
  134.4 2.2 fusion.49
  136.6 1.4 add_dynamic-update-slice_fusion.6
  138.0 1.4 add_dynamic-update-slice_fusion.7
  139.4 1.0 copy.19
  140.5 1.2 copy.20
  141.7 5.1 %collective-permute-start.1 = (bf16[2,64,2048]{2,1,0:T(8,128)(2,1)S(1)}, bf16[2,64,2048]{2,1,0:T(8,128)(2,1)}, u32[]{:S(2)}, u32[]{:S(2)}) collective-permute-start(bf16[2,64,2048]{2,1,0:T(8,128)(2,1)S(1)} %copy.20), channel_id=1, source_target_pairs={{0,112},{16,0},{32,16},{48,32},{64,48},{80,64},{96,80},{112,96},{1... | collective-permute-start | bytes 1572872 | tf_op jit(solution)/shard_map/while/body/eval_jaxpr/ppermute | solution.py:9
  146.8 5.7 %fusion.48 = f32[2,1536]{1,0:T(2,128)} fusion(bf16[2,64,2048]{2,1,0:T(8,128)(2,1)S(1)} %copy.19, bf16[1536,2048]{1,0:T(8,128)(2,1)} %get-tuple-element.317, f32[64,1536]{1,0:T(8,128)S(1)} %get-tuple-element.282), kind=kOutput, calls=%fused_computation.7.clone.1 | convolution fusion | flops 805696512 | bytes 7221248 | tf_op jit(solution)/shard_map/while/body/eval_jaxpr/dot_general | solution.py:26
  152.6 2.2 fusion.49
  154.8 1.4 add_dynamic-update-slice_fusion.6
  156.2 1.4 add_dynamic-update-slice_fusion.7
  157.6 1.0 copy.19
  158.6 1.2 copy.20
  159.8 5.1 %collective-permute-start.1 = (bf16[2,64,2048]{2,1,0:T(8,128)(2,1)S(1)}, bf16[2,64,2048]{2,1,0:T(8,128)(2,1)}, u32[]{:S(2)}, u32[]{:S(2)}) collective-permute-start(bf16[2,64,2048]{2,1,0:T(8,128)(2,1)S(1)} %copy.20), channel_id=1, source_target_pairs={{0,112},{16,0},{32,16},{48,32},{64,48},{80,64},{96,80},{112,96},{1... | collective-permute-start | bytes 1572872 | tf_op jit(solution)/shard_map/while/body/eval_jaxpr/ppermute | solution.py:9
  165.0 5.7 %fusion.48 = f32[2,1536]{1,0:T(2,128)} fusion(bf16[2,64,2048]{2,1,0:T(8,128)(2,1)S(1)} %copy.19, bf16[1536,2048]{1,0:T(8,128)(2,1)} %get-tuple-element.317, f32[64,1536]{1,0:T(8,128)S(1)} %get-tuple-element.282), kind=kOutput, calls=%fused_computation.7.clone.1 | convolution fusion | flops 805696512 | bytes 7221248 | tf_op jit(solution)/shard_map/while/body/eval_jaxpr/dot_general | solution.py:26
  170.7 2.2 fusion.49
  173.0 1.4 add_dynamic-update-slice_fusion.6
  174.4 1.4 add_dynamic-update-slice_fusion.7
  175.8 1.0 copy.19
  176.8 1.2 copy.20
  178.0 5.1 %collective-permute-start.1 = (bf16[2,64,2048]{2,1,0:T(8,128)(2,1)S(1)}, bf16[2,64,2048]{2,1,0:T(8,128)(2,1)}, u32[]{:S(2)}, u32[]{:S(2)}) collective-permute-start(bf16[2,64,2048]{2,1,0:T(8,128)(2,1)S(1)} %copy.20), channel_id=1, source_target_pairs={{0,112},{16,0},{32,16},{48,32},{64,48},{80,64},{96,80},{112,96},{1... | collective-permute-start | bytes 1572872 | tf_op jit(solution)/shard_map/while/body/eval_jaxpr/ppermute | solution.py:9
  183.2 5.7 %fusion.48 = f32[2,1536]{1,0:T(2,128)} fusion(bf16[2,64,2048]{2,1,0:T(8,128)(2,1)S(1)} %copy.19, bf16[1536,2048]{1,0:T(8,128)(2,1)} %get-tuple-element.317, f32[64,1536]{1,0:T(8,128)S(1)} %get-tuple-element.282), kind=kOutput, calls=%fused_computation.7.clone.1 | convolution fusion | flops 805696512 | bytes 7221248 | tf_op jit(solution)/shard_map/while/body/eval_jaxpr/dot_general | solution.py:26
  188.9 2.2 fusion.49
  191.2 1.4 add_dynamic-update-slice_fusion.6
  192.6 1.4 add_dynamic-update-slice_fusion.7
  194.0 5.3 %fusion.29 = f32[2,1536]{1,0:T(2,128)S(1)} fusion(bf16[2,64,2048]{2,1,0:T(8,128)(2,1)} %get-tuple-element.207, bf16[1536,2048]{1,0:T(8,128)(2,1)} %get-tuple-element.328, f32[64,1536]{1,0:T(8,128)} %convert_bitcast_fusion.3), kind=kOutput, calls=%fused_computation.19 | convolution fusion | flops 805696512 | bytes 7221248 | tf_op jit(solution)/shard_map/dot_general | solution.py:26
  199.4 3.3 %fusion.26 = f32[2,1536]{1,0:T(2,128)S(1)} fusion(bf16[2,64,2048]{2,1,0:T(8,128)(2,1)} %get-tuple-element.208, bf16[1536,2048]{1,0:T(8,128)(2,1)S(1)} %copy-done, f32[64,1536]{1,0:T(8,128)S(1)} %copy-done.1), kind=kOutput, calls=%fused_computation.18 | convolution fusion | flops 805696512 | bytes 7221248 | tf_op jit(solution)/shard_map/dot_general | solution.py:26
  202.9 15.3 %all_to_all.5 = f32[16,16,96]{2,1,0:T(8,128)S(1)} all-to-all(f32[16,16,96]{2,1,0:T(8,128)S(1)} %copy.9), channel_id=1, replica_groups=mesh['cell'=8,'idx'=16] {'idx'}, dimensions={0} | all-to-all | bytes 196608 | tf_op jit(solution)/shard_map/all_to_all | solution.py:20
  218.2 0.6 reduce_sum.61
  (73 shorter events, 1.0 us)
Async XLA Ops:
  6.5 58.7 %all-gather.2.cloned.1.call-start = ((), (), s32[]{:S(2)}) async-start(), calls=%async_computation.1 | async-start | bytes 6684672 | tf_op jit(solution)/shard_map/all_gather | solution.py:37
  66.9 17.2 %collective-permute-start = (bf16[2,64,2048]{2,1,0:T(8,128)(2,1)S(1)}, bf16[2,64,2048]{2,1,0:T(8,128)(2,1)}, u32[]{:S(2)}, u32[]{:S(2)}) collective-permute-start(bf16[2,64,2048]{2,1,0:T(8,128)(2,1)S(1)} %copy.19), channel_id=1, source_target_pairs={{0,16},{16,32},{32,48},{48,64},{64,80},{80,96},{96,112},{112,0},{1... | collective-permute-start | bytes 1572872 | tf_op jit(solution)/shard_map/while/body/eval_jaxpr/ppermute | solution.py:9
  68.2 10.9 %slice-start = ((s8[6291456]{0:T(1024)(128)(4,1)}), s8[2097152]{0:T(1024)(128)(4,1)S(1)}, s32[]{:S(2)}) async-start(s8[6291456]{0:T(1024)(128)(4,1)} %bitcast.49), calls=%async_computation.2 | async-start | bytes 4194304 | tf_op jit(solution)/shard_map/while
  69.4 14.7 %collective-permute-start.1 = (bf16[2,64,2048]{2,1,0:T(8,128)(2,1)S(1)}, bf16[2,64,2048]{2,1,0:T(8,128)(2,1)}, u32[]{:S(2)}, u32[]{:S(2)}) collective-permute-start(bf16[2,64,2048]{2,1,0:T(8,128)(2,1)S(1)} %copy.20), channel_id=1, source_target_pairs={{0,112},{16,0},{32,16},{48,32},{64,48},{80,64},{96,80},{112,96},{1... | collective-permute-start | bytes 1572872 | tf_op jit(solution)/shard_map/while/body/eval_jaxpr/ppermute | solution.py:9
  73.3 5.8 %slice-start.1 = ((s8[6291456]{0:T(1024)(128)(4,1)}), s8[4194304]{0:T(1024)(128)(4,1)S(1)}, s32[]{:S(2)}) async-start(s8[6291456]{0:T(1024)(128)(4,1)} %bitcast.49), calls=%async_computation.3 | async-start | bytes 8388608 | tf_op jit(solution)/shard_map/while
  85.1 17.9 %collective-permute-start = (bf16[2,64,2048]{2,1,0:T(8,128)(2,1)S(1)}, bf16[2,64,2048]{2,1,0:T(8,128)(2,1)}, u32[]{:S(2)}, u32[]{:S(2)}) collective-permute-start(bf16[2,64,2048]{2,1,0:T(8,128)(2,1)S(1)} %copy.19), channel_id=1, source_target_pairs={{0,16},{16,32},{32,48},{48,64},{64,80},{80,96},{96,112},{112,0},{1... | collective-permute-start | bytes 1572872 | tf_op jit(solution)/shard_map/while/body/eval_jaxpr/ppermute | solution.py:9
  85.1 12.8 %slice-start = ((s8[6291456]{0:T(1024)(128)(4,1)}), s8[2097152]{0:T(1024)(128)(4,1)S(1)}, s32[]{:S(2)}) async-start(s8[6291456]{0:T(1024)(128)(4,1)} %bitcast.49), calls=%async_computation.2 | async-start | bytes 4194304 | tf_op jit(solution)/shard_map/while
  86.3 16.7 %collective-permute-start.1 = (bf16[2,64,2048]{2,1,0:T(8,128)(2,1)S(1)}, bf16[2,64,2048]{2,1,0:T(8,128)(2,1)}, u32[]{:S(2)}, u32[]{:S(2)}) collective-permute-start(bf16[2,64,2048]{2,1,0:T(8,128)(2,1)S(1)} %copy.20), channel_id=1, source_target_pairs={{0,112},{16,0},{32,16},{48,32},{64,48},{80,64},{96,80},{112,96},{1... | collective-permute-start | bytes 1572872 | tf_op jit(solution)/shard_map/while/body/eval_jaxpr/ppermute | solution.py:9
  92.2 5.8 %slice-start.1 = ((s8[6291456]{0:T(1024)(128)(4,1)}), s8[4194304]{0:T(1024)(128)(4,1)S(1)}, s32[]{:S(2)}) async-start(s8[6291456]{0:T(1024)(128)(4,1)} %bitcast.49), calls=%async_computation.3 | async-start | bytes 8388608 | tf_op jit(solution)/shard_map/while
  104.1 17.1 %collective-permute-start = (bf16[2,64,2048]{2,1,0:T(8,128)(2,1)S(1)}, bf16[2,64,2048]{2,1,0:T(8,128)(2,1)}, u32[]{:S(2)}, u32[]{:S(2)}) collective-permute-start(bf16[2,64,2048]{2,1,0:T(8,128)(2,1)S(1)} %copy.19), channel_id=1, source_target_pairs={{0,16},{16,32},{32,48},{48,64},{64,80},{80,96},{96,112},{112,0},{1... | collective-permute-start | bytes 1572872 | tf_op jit(solution)/shard_map/while/body/eval_jaxpr/ppermute | solution.py:9
  105.0 11.2 %slice-start = ((s8[6291456]{0:T(1024)(128)(4,1)}), s8[2097152]{0:T(1024)(128)(4,1)S(1)}, s32[]{:S(2)}) async-start(s8[6291456]{0:T(1024)(128)(4,1)} %bitcast.49), calls=%async_computation.2 | async-start | bytes 4194304 | tf_op jit(solution)/shard_map/while
  106.1 15.1 %collective-permute-start.1 = (bf16[2,64,2048]{2,1,0:T(8,128)(2,1)S(1)}, bf16[2,64,2048]{2,1,0:T(8,128)(2,1)}, u32[]{:S(2)}, u32[]{:S(2)}) collective-permute-start(bf16[2,64,2048]{2,1,0:T(8,128)(2,1)S(1)} %copy.20), channel_id=1, source_target_pairs={{0,112},{16,0},{32,16},{48,32},{64,48},{80,64},{96,80},{112,96},{1... | collective-permute-start | bytes 1572872 | tf_op jit(solution)/shard_map/while/body/eval_jaxpr/ppermute | solution.py:9
  110.4 5.8 %slice-start.1 = ((s8[6291456]{0:T(1024)(128)(4,1)}), s8[4194304]{0:T(1024)(128)(4,1)S(1)}, s32[]{:S(2)}) async-start(s8[6291456]{0:T(1024)(128)(4,1)} %bitcast.49), calls=%async_computation.3 | async-start | bytes 8388608 | tf_op jit(solution)/shard_map/while
  122.3 17.2 %collective-permute-start = (bf16[2,64,2048]{2,1,0:T(8,128)(2,1)S(1)}, bf16[2,64,2048]{2,1,0:T(8,128)(2,1)}, u32[]{:S(2)}, u32[]{:S(2)}) collective-permute-start(bf16[2,64,2048]{2,1,0:T(8,128)(2,1)S(1)} %copy.19), channel_id=1, source_target_pairs={{0,16},{16,32},{32,48},{48,64},{64,80},{80,96},{96,112},{112,0},{1... | collective-permute-start | bytes 1572872 | tf_op jit(solution)/shard_map/while/body/eval_jaxpr/ppermute | solution.py:9
  122.3 12.1 %slice-start = ((s8[6291456]{0:T(1024)(128)(4,1)}), s8[2097152]{0:T(1024)(128)(4,1)S(1)}, s32[]{:S(2)}) async-start(s8[6291456]{0:T(1024)(128)(4,1)} %bitcast.49), calls=%async_computation.2 | async-start | bytes 4194304 | tf_op jit(solution)/shard_map/while
  123.5 16.0 %collective-permute-start.1 = (bf16[2,64,2048]{2,1,0:T(8,128)(2,1)S(1)}, bf16[2,64,2048]{2,1,0:T(8,128)(2,1)}, u32[]{:S(2)}, u32[]{:S(2)}) collective-permute-start(bf16[2,64,2048]{2,1,0:T(8,128)(2,1)S(1)} %copy.20), channel_id=1, source_target_pairs={{0,112},{16,0},{32,16},{48,32},{64,48},{80,64},{96,80},{112,96},{1... | collective-permute-start | bytes 1572872 | tf_op jit(solution)/shard_map/while/body/eval_jaxpr/ppermute | solution.py:9
  128.6 5.8 %slice-start.1 = ((s8[6291456]{0:T(1024)(128)(4,1)}), s8[4194304]{0:T(1024)(128)(4,1)S(1)}, s32[]{:S(2)}) async-start(s8[6291456]{0:T(1024)(128)(4,1)} %bitcast.49), calls=%async_computation.3 | async-start | bytes 8388608 | tf_op jit(solution)/shard_map/while
  140.5 17.1 %collective-permute-start = (bf16[2,64,2048]{2,1,0:T(8,128)(2,1)S(1)}, bf16[2,64,2048]{2,1,0:T(8,128)(2,1)}, u32[]{:S(2)}, u32[]{:S(2)}) collective-permute-start(bf16[2,64,2048]{2,1,0:T(8,128)(2,1)S(1)} %copy.19), channel_id=1, source_target_pairs={{0,16},{16,32},{32,48},{48,64},{64,80},{80,96},{96,112},{112,0},{1... | collective-permute-start | bytes 1572872 | tf_op jit(solution)/shard_map/while/body/eval_jaxpr/ppermute | solution.py:9
  140.5 12.1 %slice-start = ((s8[6291456]{0:T(1024)(128)(4,1)}), s8[2097152]{0:T(1024)(128)(4,1)S(1)}, s32[]{:S(2)}) async-start(s8[6291456]{0:T(1024)(128)(4,1)} %bitcast.49), calls=%async_computation.2 | async-start | bytes 4194304 | tf_op jit(solution)/shard_map/while
  141.7 15.9 %collective-permute-start.1 = (bf16[2,64,2048]{2,1,0:T(8,128)(2,1)S(1)}, bf16[2,64,2048]{2,1,0:T(8,128)(2,1)}, u32[]{:S(2)}, u32[]{:S(2)}) collective-permute-start(bf16[2,64,2048]{2,1,0:T(8,128)(2,1)S(1)} %copy.20), channel_id=1, source_target_pairs={{0,112},{16,0},{32,16},{48,32},{64,48},{80,64},{96,80},{112,96},{1... | collective-permute-start | bytes 1572872 | tf_op jit(solution)/shard_map/while/body/eval_jaxpr/ppermute | solution.py:9
  146.8 5.8 %slice-start.1 = ((s8[6291456]{0:T(1024)(128)(4,1)}), s8[4194304]{0:T(1024)(128)(4,1)S(1)}, s32[]{:S(2)}) async-start(s8[6291456]{0:T(1024)(128)(4,1)} %bitcast.49), calls=%async_computation.3 | async-start | bytes 8388608 | tf_op jit(solution)/shard_map/while
  158.6 17.2 %collective-permute-start = (bf16[2,64,2048]{2,1,0:T(8,128)(2,1)S(1)}, bf16[2,64,2048]{2,1,0:T(8,128)(2,1)}, u32[]{:S(2)}, u32[]{:S(2)}) collective-permute-start(bf16[2,64,2048]{2,1,0:T(8,128)(2,1)S(1)} %copy.19), channel_id=1, source_target_pairs={{0,16},{16,32},{32,48},{48,64},{64,80},{80,96},{96,112},{112,0},{1... | collective-permute-start | bytes 1572872 | tf_op jit(solution)/shard_map/while/body/eval_jaxpr/ppermute | solution.py:9
  158.6 12.1 %slice-start = ((s8[6291456]{0:T(1024)(128)(4,1)}), s8[2097152]{0:T(1024)(128)(4,1)S(1)}, s32[]{:S(2)}) async-start(s8[6291456]{0:T(1024)(128)(4,1)} %bitcast.49), calls=%async_computation.2 | async-start | bytes 4194304 | tf_op jit(solution)/shard_map/while
  159.8 16.0 %collective-permute-start.1 = (bf16[2,64,2048]{2,1,0:T(8,128)(2,1)S(1)}, bf16[2,64,2048]{2,1,0:T(8,128)(2,1)}, u32[]{:S(2)}, u32[]{:S(2)}) collective-permute-start(bf16[2,64,2048]{2,1,0:T(8,128)(2,1)S(1)} %copy.20), channel_id=1, source_target_pairs={{0,112},{16,0},{32,16},{48,32},{64,48},{80,64},{96,80},{112,96},{1... | collective-permute-start | bytes 1572872 | tf_op jit(solution)/shard_map/while/body/eval_jaxpr/ppermute | solution.py:9
  165.0 5.8 %slice-start.1 = ((s8[6291456]{0:T(1024)(128)(4,1)}), s8[4194304]{0:T(1024)(128)(4,1)S(1)}, s32[]{:S(2)}) async-start(s8[6291456]{0:T(1024)(128)(4,1)} %bitcast.49), calls=%async_computation.3 | async-start | bytes 8388608 | tf_op jit(solution)/shard_map/while
  176.8 17.1 %collective-permute-start = (bf16[2,64,2048]{2,1,0:T(8,128)(2,1)S(1)}, bf16[2,64,2048]{2,1,0:T(8,128)(2,1)}, u32[]{:S(2)}, u32[]{:S(2)}) collective-permute-start(bf16[2,64,2048]{2,1,0:T(8,128)(2,1)S(1)} %copy.19), channel_id=1, source_target_pairs={{0,16},{16,32},{32,48},{48,64},{64,80},{80,96},{96,112},{112,0},{1... | collective-permute-start | bytes 1572872 | tf_op jit(solution)/shard_map/while/body/eval_jaxpr/ppermute | solution.py:9
  176.8 12.1 %slice-start = ((s8[6291456]{0:T(1024)(128)(4,1)}), s8[2097152]{0:T(1024)(128)(4,1)S(1)}, s32[]{:S(2)}) async-start(s8[6291456]{0:T(1024)(128)(4,1)} %bitcast.49), calls=%async_computation.2 | async-start | bytes 4194304 | tf_op jit(solution)/shard_map/while
  178.0 15.9 %collective-permute-start.1 = (bf16[2,64,2048]{2,1,0:T(8,128)(2,1)S(1)}, bf16[2,64,2048]{2,1,0:T(8,128)(2,1)}, u32[]{:S(2)}, u32[]{:S(2)}) collective-permute-start(bf16[2,64,2048]{2,1,0:T(8,128)(2,1)S(1)} %copy.20), channel_id=1, source_target_pairs={{0,112},{16,0},{32,16},{48,32},{64,48},{80,64},{96,80},{112,96},{1... | collective-permute-start | bytes 1572872 | tf_op jit(solution)/shard_map/while/body/eval_jaxpr/ppermute | solution.py:9
  183.2 5.8 %slice-start.1 = ((s8[6291456]{0:T(1024)(128)(4,1)}), s8[4194304]{0:T(1024)(128)(4,1)S(1)}, s32[]{:S(2)}) async-start(s8[6291456]{0:T(1024)(128)(4,1)} %bitcast.49), calls=%async_computation.3 | async-start | bytes 8388608 | tf_op jit(solution)/shard_map/while
  194.0 5.4 %copy-start.2 = (f32[16,1536]{1,0:T(8,128)S(1)}, f32[16,1536]{1,0:T(8,128)}, u32[]{:S(2)}) copy-start(f32[16,1536]{1,0:T(8,128)} %get-tuple-element.206) | copy-start | bytes 294916
  194.0 5.4 %copy-start = (bf16[1536,2048]{1,0:T(8,128)(2,1)S(1)}, bf16[1536,2048]{1,0:T(8,128)(2,1)}, u32[]{:S(2)}) copy-start(bf16[1536,2048]{1,0:T(8,128)(2,1)} %get-tuple-element.328) | copy-start | bytes 18874372
  194.0 5.4 %copy-start.1 = (f32[64,1536]{1,0:T(8,128)S(1)}, f32[64,1536]{1,0:T(8,128)}, u32[]{:S(2)}) copy-start(f32[64,1536]{1,0:T(8,128)} %convert_bitcast_fusion.2) | copy-start | bytes 1179652
Sparse Core Ops, SparseCore 0:
  8.9 56.2 all-gather.1
where the time goes:
time: 227 us; the launch traced here: 226 us
  matrix products  64.2 us (28%)
  waiting for transfers between devices  53.2 us (23%)
  starting transfers between devices  36.3 us (16%)
  other arithmetic  22.4 us (10%)
  local copies, waits for them, and re-layouts  20.4 us (9%)
  blocking collectives  15.3 us (7%)
  between operations  13.5 us (6%)
    dot_general x16, matrix products, contract(): lax.dot_general(slab.reshape(outputs * inner, width), whole, (((1,), (1,)...  64.2 us
    all_gather x1, waiting for transfers between devices, shards(): whole = lax.all_gather(coeffs, 'idx', axis=1, tiled=True)  52.5 us
    ppermute x14, starting transfers between devices, passed_along(): lax.ppermute(shard, axis, [(i, (i + by) % devices) for i in range(devices)])  36.3 us
    dynamic_update_slice x16, other arithmetic, deposit(): acc = lax.dynamic_update_slice(acc, current + piece, (place, jnp.int32(0)))  19.8 us
    another operation x14, local copies, waits for them, and re-layouts  15.6 us
    all_to_all x1, blocking collectives, sum_at_owner(): lax.all_to_all(split_up(shard, dim, devices), axis, 0, 0, tiled=True)  15.3 us
  transfers between devices with their start and end apart: 15, of which 1 were waited for; matrix products, arithmetic and copies ran while one was open for 40% of the time, Pallas kernels for 0%

commit v1 on v0

v1 whole, which is shorter than its diff:
```python
import jax
import jax.numpy as jnp
from jax import lax
from jax.experimental import pallas as pl
from jax.experimental.pallas import tpu as pltpu
from jax.sharding import PartitionSpec as P

F32 = jnp.float32
BF16 = jnp.bfloat16
NX = 4
NY = 4
ROW_OF_DY = {0: 0, 1: 1, 3: 2, 2: 3}
PIECES = (0, 1, 3, 2)
ONWARD_UP = (0, 3)
ONWARD_DOWN = (1, 2)


def flip(bit, other):
    return 1 - bit if other else bit


def kernel(
    x_hbm, t_hbm, o_ref,
    xin, outbox, slab, xi, xj, outp, stage, arrived,
    in_sem, t_sem, y_send, z_send, x_send, pair_send, out_send,
    slab_recv, xi_recv, xj_recv, out_recv,
):
    cell = lax.axis_index("cell")
    idx = lax.axis_index("idx")
    zh = cell // NY
    y = cell % NY
    core = idx % 2
    x = (idx // 2) % NX
    zl = idx // (2 * NX)
    cells, width = x_hbm.shape
    owners = lax.axis_size("idx")
    own = cells // owners

    def device(dx=0, dy=0, e=0, other_core=0):
        return {
            "cell": flip(zh, e // 2) * NY + (y + dy) % NY,
            "idx": (flip(zl, e % 2) * NX + (x + dx) % NX) * 2 + flip(core, other_core),
        }

    def copy_to(src, dst, send, recv, dev):
        return pltpu.make_async_remote_copy(
            src_ref=src, dst_ref=dst, send_sem=send, recv_sem=recv,
            device_id=dev, device_id_type=pl.DeviceIdType.MESH,
        )

    x_in = pltpu.make_async_copy(x_hbm, xin, in_sem)
    x_in.start()

    def part_of(e):
        return slab.at[0] if e == 0 else outbox.at[e - 1]

    for e in PIECES:
        for dx in range(NX):
            block = (flip(zl, e % 2) * NX + (x + dx) % NX) * 2 + flip(zh, e // 2)
            pltpu.make_async_copy(
                t_hbm.at[:, pl.ds(pl.multiple_of(block * width, width), width)],
                part_of(e).at[:, pl.ds(dx * width, width)],
                t_sem.at[e],
            ).start()

    barrier = pltpu.get_barrier_semaphore()
    peers = [
        device(dx=dx, e=e, other_core=oc)
        for e in range(4) for dx in range(NX) for oc in range(2)
        if (e, dx, oc) != (0, 0, 0)
    ] + [device(dy=1), device(dy=3)]
    for peer in peers:
        pl.semaphore_signal(
            barrier, inc=1, device_id=peer, device_id_type=pl.DeviceIdType.MESH
        )

    x_in.wait()
    for t in range(cells // width):
        xi[0, :, t * width : (t + 1) * width] = jnp.transpose(
            xin[t * width : (t + 1) * width, :]
        )

    source = core == zh

    @pl.when(source)
    def _():
        xj[0, :width, :] = xi[0]

    for e in PIECES:
        pltpu.make_async_copy(part_of(e), part_of(e), t_sem.at[e]).wait()

    pl.semaphore_wait(barrier, len(peers))

    def y_copy(dy, e, up):
        n = (0 if up else 6) + (PIECES.index(e) if dy == 0 else 4 + (ONWARD_UP if up else ONWARD_DOWN).index(e))
        there = (dy - (1 if up else -1)) % NY
        return copy_to(
            slab.at[dy * 4 + e], slab.at[there * 4 + e],
            y_send.at[n], slab_recv.at[there * 4 + e], device(dy=1 if up else 3),
        )

    def z_copy_t(e):
        return copy_to(
            outbox.at[e - 1], slab.at[e], z_send.at[e - 1], slab_recv.at[e], device(e=e)
        )

    def z_copy_x(e):
        return copy_to(xi.at[0], xi.at[e], z_send.at[2 + e], xi_recv.at[e], device(e=e))

    def block_of(hr, dx):
        return xj.at[hr, pl.ds(dx * width, width)]

    def x_copy(hr, dx):
        return copy_to(
            xi.at[2 * hr], block_of(hr, NX - dx),
            x_send.at[hr * 3 + dx - 1], xj_recv.at[hr * 4 + NX - dx], device(dx=dx),
        )

    def pair_copy(hr, dx):
        src = xi.at[2 * hr] if dx == 0 else block_of(hr, dx)
        return copy_to(
            src, block_of(hr, dx),
            pair_send.at[hr * 4 + dx], xj_recv.at[hr * 4 + dx], device(other_core=1),
        )

    def got_slab(dy, e):
        there = slab.at[dy * 4 + e]
        pltpu.make_async_copy(there, there, slab_recv.at[dy * 4 + e]).wait()

    def got_xi(e):
        pltpu.make_async_copy(xi.at[e], xi.at[e], xi_recv.at[e]).wait()

    def got_xj(hr, dx):
        there = block_of(hr, dx)
        pltpu.make_async_copy(there, there, xj_recv.at[hr * 4 + dx]).wait()

    def y_own(e):
        y_copy(0, e, True).start()
        y_copy(0, e, False).start()

    def take_xj(hr, dxs):
        @pl.when(source)
        def _():
            for dx in dxs:
                got_xj(hr, dx)
                pair_copy(hr, dx).start()

    def have_xj(hr):
        @pl.when(jnp.logical_not(source))
        def _():
            for dx in range(NX):
                got_xj(hr, dx)

    def unit(dy, eh, hr):
        row = ROW_OF_DY[dy] * 4 + eh * 2

        def tile(n, _):
            cols = pl.ds(pl.multiple_of(n * 256, 256), 256)
            w = xj[hr, :, cols]
            total = None
            for el in range(2):
                mixed = jnp.dot(slab[dy * 4 + eh * 2 + el], w, preferred_element_type=F32)
                rows = xi[hr * 2 + el, :, cols].astype(F32)
                terms = mixed.reshape(2, width, 256) * rows[None]
                part = jnp.sum(terms.reshape(2, width // 8, 8, 256), axis=1)
                total = part if total is None else total + part
            outp[hr, row : row + 2, cols] = jnp.sum(total, axis=1)
            return 0

        lax.fori_loop(0, cells // 256, tile, 0)

    def send_out(b):
        for hr in range(2):
            rows = outp[hr, b * 8 : b * 8 + 8, :]
            for q in range(owners):
                first = q * own // 128 * 128
                shift = q * own - first
                window = rows[:, first : first + 256] if first + 256 <= cells else rows[:, first : first + 128]
                if shift:
                    window = pltpu.roll(window, window.shape[1] - shift, 1)
                stage[b, hr * owners + q] = window[:, :128]

        def send(j, _):
            hr = j // owners
            q = (idx + j) % owners
            copy_to(
                stage.at[b, hr * owners + q], arrived.at[b, hr * owners + idx],
                out_send.at[b], out_recv.at[b],
                {"cell": (zh + hr - 2 * zh * hr) * NY + y, "idx": q},
            ).start()
            return 0

        lax.fori_loop(1, 2 * owners, send, 0)
        arrived[b, idx] = stage[b, idx]

    def all_but_one(ref, b):
        return ref.at[b, pl.ds(0, 2 * owners - 1)]

    y_own(0)

    @pl.when(source)
    def _():
        for e in (1, 3, 2):
            z_copy_t(e).start()
        for dx in (1, 3, 2):
            x_copy(0, dx).start()
        pair_copy(0, 0).start()
        for e in (1, 3, 2):
            z_copy_x(e).start()

    @pl.when(jnp.logical_not(source))
    def _():
        z_copy_x(2).start()
        for e in (1, 3, 2):
            z_copy_t(e).start()
        for e in (1, 3):
            z_copy_x(e).start()

    got_slab(0, 1)
    y_own(1)
    got_slab(0, 3)
    y_own(3)
    take_xj(0, (1, 3))
    got_slab(3, 0)
    y_copy(3, 0, True).start()
    got_xi(2)

    @pl.when(source)
    def _():
        for dx in (1, 3, 2):
            x_copy(1, dx).start()
        pair_copy(1, 0).start()
        xj[1, :width, :] = xi[2]

    got_slab(0, 2)
    y_own(2)
    take_xj(0, (2,))
    got_slab(1, 1)
    y_copy(1, 1, False).start()
    got_xi(1)
    have_xj(0)
    unit(0, 0, 0)
    unit(0, 1, 0)
    got_slab(3, 1)
    got_slab(1, 0)
    unit(1, 0, 0)
    take_xj(1, (1, 3))
    unit(3, 0, 0)
    got_slab(3, 3)
    y_copy(3, 3, True).start()
    take_xj(1, (2,))
    got_xi(3)
    have_xj(1)
    unit(0, 0, 1)
    unit(0, 1, 1)
    got_slab(1, 2)
    y_copy(1, 2, False).start()
    unit(1, 0, 1)
    unit(3, 0, 1)
    got_slab(1, 3)
    unit(1, 1, 0)
    unit(1, 1, 1)
    send_out(0)
    got_slab(3, 2)
    unit(3, 1, 0)
    unit(3, 1, 1)
    got_slab(2, 0)
    got_slab(2, 1)
    unit(2, 0, 0)
    unit(2, 0, 1)
    got_slab(2, 3)
    got_slab(2, 2)
    unit(2, 1, 0)
    unit(2, 1, 1)
    send_out(1)

    for b in range(2):
        pltpu.make_async_copy(all_but_one(arrived, b), all_but_one(arrived, b), out_recv.at[b]).wait()
        same = jnp.sum(arrived[b, :owners], axis=0)
        crossed = jnp.sum(arrived[b, owners:], axis=0)
        for r in range(4):
            dy = [d for d, place in ROW_OF_DY.items() if place == b * 2 + r // 2][0]
            eh = r % 2
            k = (flip(zh, eh) * NY + (y + dy) % NY) * 2
            for kk in range(2):
                a = r * 2 + kk
                c = (r ^ 1) * 2 + kk
                o_ref[pl.ds(k + kk, 1), :] = (same[a : a + 1] + crossed[c : c + 1])[:, :own]

    for e in PIECES:
        y_copy(0, e, True).wait_send()
        y_copy(0, e, False).wait_send()
    for e in ONWARD_UP:
        y_copy(3, e, True).wait_send()
    for e in ONWARD_DOWN:
        y_copy(1, e, False).wait_send()
    for e in (1, 2, 3):
        z_copy_t(e).wait_send()
        z_copy_x(e).wait_send()

    @pl.when(source)
    def _():
        for hr in range(2):
            for dx in range(NX):
                pair_copy(hr, dx).wait_send()
                if dx:
                    x_copy(hr, dx).wait_send()

    for b in range(2):
        pltpu.make_async_copy(all_but_one(stage, b), all_but_one(stage, b), out_send.at[b]).wait()


def shards(coeffs, tensor):
    cells, width = coeffs.shape
    outputs, inner, full = tensor.shape
    owners = lax.axis_size("idx")
    rows = outputs * inner
    return pl.pallas_call(
        kernel,
        out_shape=jax.ShapeDtypeStruct((16, cells // owners), F32),
        in_specs=[pl.BlockSpec(memory_space=pl.ANY)] * 2,
        out_specs=pl.BlockSpec(memory_space=pltpu.VMEM),
        scratch_shapes=[
            pltpu.VMEM((cells, width), BF16),
            pltpu.VMEM((3, rows, NX * width), BF16),
            pltpu.VMEM((16, rows, NX * width), BF16),
            pltpu.VMEM((4, width, cells), BF16),
            pltpu.VMEM((2, NX * width, cells), BF16),
            pltpu.VMEM((2, 16, cells), F32),
            pltpu.VMEM((2, 2 * owners, 8, 128), F32),
            pltpu.VMEM((2, 2 * owners, 8, 128), F32),
            pltpu.SemaphoreType.DMA,
            pltpu.SemaphoreType.DMA((4,)),
            pltpu.SemaphoreType.DMA((12,)),
            pltpu.SemaphoreType.DMA((6,)),
            pltpu.SemaphoreType.DMA((6,)),
            pltpu.SemaphoreType.DMA((8,)),
            pltpu.SemaphoreType.DMA((2,)),
            pltpu.SemaphoreType.DMA((16,)),
            pltpu.SemaphoreType.DMA((4,)),
            pltpu.SemaphoreType.DMA((8,)),
            pltpu.SemaphoreType.DMA((2,)),
        ],
        compiler_params=pltpu.CompilerParams(
            collective_id=0, has_side_effects=True, vmem_limit_bytes=48 * 1024 * 1024
        ),
    )(coeffs, tensor.reshape(rows, full))


def solution(mesh):
    return jax.shard_map(
        shards,
        mesh=mesh,
        in_specs=(P("cell", "idx"), P("cell", "idx", None)),
        out_specs=P(None, ("cell", "idx")),
        check_vma=False,
    )
```

time: 227 us -> 78.5 us (0.35)
  Pallas kernels: 0 us -> 75.5 us
  matrix products: 64.2 us -> 0 us
  waiting for transfers between devices: 53.2 us -> 0 us
  starting transfers between devices: 36.3 us -> 0 us
  other arithmetic: 22.4 us -> 0 us
  local copies, waits for them, and re-layouts: 20.4 us -> 2.82 us
  blocking collectives: 15.3 us -> 0 us
  between operations: 13.5 us -> 0.01 us
    pallas_call x0 -> x1, Pallas kernels: none -> 75.5 us  [shards(): pl.pallas_call(kernel, out_shape=jax.ShapeDtypeStruct((16, cells // owner...]
    dot_general x16 -> x0, matrix products: 64.2 us -> none  [contract(): lax.dot_general(slab.reshape(outputs * inner, width), whole, (((1,), (1,)...]
    all_gather x1 -> x0, waiting for transfers between devices: 52.5 us -> none  [shards(): whole = lax.all_gather(coeffs, 'idx', axis=1, tiled=True)]
    ppermute x14 -> x0, starting transfers between devices: 36.3 us -> none  [passed_along(): lax.ppermute(shard, axis, [(i, (i + by) % devices) for i in range(devices)])]
    dynamic_update_slice x16 -> x0, other arithmetic: 19.8 us -> none  [deposit(): acc = lax.dynamic_update_slice(acc, current + piece, (place, jnp.int32(0)))]
    another operation x14 -> x0, local copies, waits for them, and re-layouts: 15.6 us -> none
    all_to_all x1 -> x0, blocking collectives: 15.3 us -> none  [sum_at_owner(): lax.all_to_all(split_up(shard, dim, devices), axis, 0, 0, tiled=True)]
    slice x2 -> x0, local copies, waits for them, and re-layouts: 3.59 us -> none  [the longest x1 2.3 us: shards(): tensor[:, half:]]
  transfers between devices with their start and end apart: 15 -> 0, of which waited for: 1 -> 0; matrix products, arithmetic and copies ran while one was open for 40% -> 0% of each run, Pallas kernels for 0% -> 0%
where the time goes in v1:
time: 78.5 us; the launch traced here: 78.3 us
  Pallas kernels  75.5 us (96%)
  local copies, waits for them, and re-layouts  2.82 us (4%)
    pallas_call x1, Pallas kernels, shards(): pl.pallas_call(kernel, out_shape=jax.ShapeDtypeStruct((16, cells // owner...  75.5 us
    unnamed x5, local copies, waits for them, and re-layouts  2.82 us

profile of v1, /device:TPU:1, one launch (start us, length us, event | category | flops | bytes accessed | tf_op | source)
XLA Modules:
  0.0 78.3 jit_solution(2768567228446304829)
XLA Ops:
  0.0 0.0 copy-start
  0.0 1.2 %copy-done = bf16[2,128,2048]{2,1,0:T(8,128)(2,1)S(1)} copy-done((bf16[2,128,2048]{2,1,0:T(8,128)(2,1)S(1)}, bf16[2,128,2048]{2,1,0:T(8,128)(2,1)}, u32[]{:S(2)}) %copy-start) | copy-done | bytes 1048600
  1.2 0.0 copy-start.1
  1.2 1.0 %copy-done.1 = bf16[1536,128]{1,0:T(8,128)(2,1)S(1)} copy-done((bf16[1536,128]{1,0:T(8,128)(2,1)S(1)}, bf16[1536,128]{1,0:T(8,128)(2,1)}, u32[]{:S(2)}) %copy-start.1) | copy-done | bytes 393240
  2.2 75.5 %shard_map.28 = f32[16,96]{1,0:T(8,128)S(1)} custom-call(bf16[1536,128]{1,0:T(8,128)(2,1)S(1)} %copy-done.1, bf16[256,2048]{1,0:T(8,128)(2,1)S(1)} %bitcast.1), custom_call_target="tpu_custom_call" | custom-call | tf_op jit(solution)/shard_map/pallas_call | solution.py:318
  77.7 0.6 copy.4
Async XLA Ops:
  0.0 1.2 %copy-start = (bf16[2,128,2048]{2,1,0:T(8,128)(2,1)S(1)}, bf16[2,128,2048]{2,1,0:T(8,128)(2,1)}, u32[]{:S(2)}) copy-start(bf16[2,128,2048]{2,1,0:T(8,128)(2,1)} %param.3) | copy-start | bytes 3145732
  1.2 1.0 %copy-start.1 = (bf16[1536,128]{1,0:T(8,128)(2,1)S(1)}, bf16[1536,128]{1,0:T(8,128)(2,1)}, u32[]{:S(2)}) copy-start(bf16[1536,128]{1,0:T(8,128)(2,1)} %x_hbm.1) | copy-start | bytes 1179652

commit v2 on v1

v2 whole, which is shorter than its diff:
```python
import jax
import jax.numpy as jnp
from jax import lax
from jax.experimental import pallas as pl
from jax.experimental.pallas import tpu as pltpu
from jax.sharding import PartitionSpec as P

F32 = jnp.float32
BF16 = jnp.bfloat16
NX = 4
NY = 4
ROW_OF_DY = {0: 0, 1: 1, 3: 2, 2: 3}


def flip(bit, other):
    return 1 - bit if other else bit


def kernel(
    x_hbm, t_hbm, o_ref,
    xin, outbox, passing, slab, xi, xj, outp, stage, arrived,
    in_sem, t_sem, y_send, z_send, x_send, pair_send, out_send,
    slab_recv, pass_recv, xi_recv, xj_recv, out_recv, ready, pair_ready,
):
    cell = lax.axis_index("cell")
    idx = lax.axis_index("idx")
    zh = cell // NY
    y = cell % NY
    core = idx % 2
    x = (idx // 2) % NX
    zl = idx // (2 * NX)
    cells, width = x_hbm.shape
    line = NX * width
    owners = lax.axis_size("idx")
    own = cells // owners

    def device(dx=0, dy=0, e=0, other_core=0):
        return {
            "cell": flip(zh, e // 2) * NY + (y + dy) % NY,
            "idx": (flip(zl, e % 2) * NX + (x + dx) % NX) * 2 + flip(core, other_core),
        }

    def copy_to(src, dst, send, recv, dev):
        return pltpu.make_async_remote_copy(
            src_ref=src, dst_ref=dst, send_sem=send, recv_sem=recv,
            device_id=dev, device_id_type=pl.DeviceIdType.MESH,
        )

    def signal(sem, dev):
        pl.semaphore_signal(sem, inc=1, device_id=dev, device_id_type=pl.DeviceIdType.MESH)

    barrier = pltpu.get_barrier_semaphore()
    peers = [device(dy=1), device(dy=3), device(other_core=1)]
    peers += [device(dx=dx) for dx in (1, 2, 3)] + [device(e=e) for e in (1, 2, 3)]
    for peer in peers:
        signal(barrier, peer)

    x_in = pltpu.make_async_copy(x_hbm, xin, in_sem)
    x_in.start()

    def part_of(eh, kk):
        return outbox.at[kk] if eh else slab.at[kk]

    for eh in range(2):
        for kk in range(2):
            for el in range(2):
                for dx in range(NX):
                    block = (flip(zl, el) * NX + (x + dx) % NX) * 2 + flip(zh, eh)
                    pltpu.make_async_copy(
                        t_hbm.at[pl.ds(kk * width, width), pl.ds(pl.multiple_of(block * width, width), width)],
                        part_of(eh, kk).at[:, pl.ds(el * line + dx * width, width)],
                        t_sem.at[eh * 2 + kk],
                    ).start()

    x_in.wait()
    for t in range(cells // width):
        xi[0, :, t * width : (t + 1) * width] = jnp.transpose(
            xin[t * width : (t + 1) * width, :]
        )

    source = core == zh

    def on_source(f):
        pl.when(source)(f)

    def on_other(f):
        pl.when(jnp.logical_not(source))(f)

    @on_source
    def _():
        xj[0, :width, :] = xi[0]

    for eh in range(2):
        for kk in range(2):
            pltpu.make_async_copy(part_of(eh, kk), part_of(eh, kk), t_sem.at[eh * 2 + kk]).wait()

    pl.semaphore_wait(barrier, len(peers))

    for dx in (1, 2, 3):
        signal(ready, device(dx=dx))

    def slot(dy, eh, kk):
        return dy * 4 + eh * 2 + kk

    def y_copy(dy, eh, kk, up):
        n = (0 if up else 6) + (eh * 2 + kk if dy == 0 else 4 + eh)
        there = slot((dy - (1 if up else -1)) % NY, eh, kk)
        return copy_to(
            slab.at[slot(dy, eh, kk)], slab.at[there],
            y_send.at[n], slab_recv.at[there], device(dy=1 if up else 3),
        )

    def block_of(hr, el, dx):
        return xj.at[hr, pl.ds(el * line + dx * width, width)]

    def half_of(hr, el, part):
        return xj.at[hr, pl.ds(el * line + 2 * width + part * (width // 2), width // 2)]

    def number(hr, el, dx):
        return (hr * 2 + el) * NX + dx

    def z_copy_t(kk):
        return copy_to(outbox.at[kk], passing.at[kk], z_send.at[kk], pass_recv.at[kk], device(e=3 if kk else 1))

    def z_onward_t(kk):
        there = slot(0, 1, kk)
        return copy_to(
            passing.at[kk], slab.at[there], z_send.at[2 + kk], slab_recv.at[there], device(e=1 if kk else 3)
        )

    def z_onward_x(hr):
        return copy_to(block_of(hr, 1, 0), xi.at[1], z_send.at[5 + hr], xi_recv, device(e=1 if hr else 3))

    def z_copy_j(e):
        hr = e // 2
        return copy_to(
            xi.at[0], block_of(hr, 1, 0), z_send.at[4], xj_recv.at[number(hr, 1, 0)], device(e=e)
        )

    def first_of(hr, el):
        return block_of(hr, el, 0) if el else xi.at[hr]

    def x_copy(hr, el, dx):
        n = number(hr, el, 0 if dx == 1 else 1)
        there = NX - dx
        return copy_to(
            first_of(hr, el), block_of(hr, el, there),
            x_send.at[n], xj_recv.at[number(hr, el, there)], device(dx=dx),
        )

    def x_onward(hr, el, dx):
        part = 0 if dx == 1 else 1
        src = xj.at[hr, pl.ds(el * line + dx * width + part * (width // 2), width // 2)]
        return copy_to(
            src, half_of(hr, el, part), x_send.at[number(hr, el, 2 + part)],
            xj_recv.at[number(hr, el, 2)], device(dx=NX - dx),
        )

    def pair_copy(hr, el, dx):
        src = first_of(hr, el) if dx == 0 else block_of(hr, el, dx)
        n = number(hr, el, dx)
        return copy_to(
            src, block_of(hr, el, dx), pair_send.at[n], xj_recv.at[n], device(other_core=1)
        )

    def got_slab(dy, eh, kk):
        there = slab.at[slot(dy, eh, kk)]
        pltpu.make_async_copy(there, there, slab_recv.at[slot(dy, eh, kk)]).wait()

    def got_passing(kk):
        pltpu.make_async_copy(passing.at[kk], passing.at[kk], pass_recv.at[kk]).wait()

    def got_xi():
        pltpu.make_async_copy(xi.at[1], xi.at[1], xi_recv).wait()

    def got_xj(hr, el, dx):
        there = block_of(hr, el, dx)
        pltpu.make_async_copy(there, there, xj_recv.at[number(hr, el, dx)]).wait()

    def y_own(eh, kk):
        y_copy(0, eh, kk, True).start()
        y_copy(0, eh, 1 - kk, False).start()

    def y_onward(eh):
        y_copy(3, eh, 0, True).start()
        y_copy(1, eh, 1, False).start()

    def spread(hr, el):
        x_copy(hr, el, 1).start()
        x_copy(hr, el, 3).start()
        pair_copy(hr, el, 0).start()

    def start_group(hr, el):
        @on_source
        def _():
            if el:
                got_xj(hr, el, 0)
            elif hr:
                got_xi()
            spread(hr, el)
            if hr and not el:
                xj[1, :width, :] = xi[1]

    def pass_on(hr, el):
        @on_source
        def _():
            for dx in (1, 3):
                got_xj(hr, el, dx)
                x_onward(hr, el, dx).start()
                pair_copy(hr, el, dx).start()

    def end_group(hr, el):
        @on_source
        def _():
            got_xj(hr, el, 2)
            pair_copy(hr, el, 2).start()

    def have_group(hr, el):
        @on_other
        def _():
            for dx in range(NX):
                got_xj(hr, el, dx)

    begun = set()

    def unit(pieces, hr, els):
        deep = pl.ds(els[0] * line, len(els) * line)

        def tile(n, _):
            cols = pl.ds(pl.multiple_of(n * 256, 256), 256)
            w = xj[hr, deep, cols]
            rows = xi[hr, :, cols].astype(F32)
            for dy, eh in pieces:
                at = slot(dy, eh, 0)
                left = slab[at : at + 2, :, deep].reshape(2 * width, len(els) * line)
                mixed = jnp.dot(left, w, preferred_element_type=F32)
                terms = mixed.reshape(2, width, 256) * rows[None]
                part = jnp.sum(terms.reshape(2, width // 8, 8, 256), axis=1)
                out = jnp.sum(part, axis=1)
                row = ROW_OF_DY[dy] * 4 + eh * 2
                if (dy, eh, hr) in begun:
                    out = out + outp[hr, row : row + 2, cols]
                outp[hr, row : row + 2, cols] = out
            return 0

        lax.fori_loop(0, cells // 256, tile, 0, unroll=True)
        begun.update((dy, eh, hr) for dy, eh in pieces)

    def send_out(b):
        for hr in range(2):
            rows = outp[hr, b * 8 : b * 8 + 8, :]
            for q in range(owners):
                first = q * own // 128 * 128
                shift = q * own - first
                window = rows[:, first : first + 256] if first + 256 <= cells else rows[:, first : first + 128]
                if shift:
                    window = pltpu.roll(window, window.shape[1] - shift, 1)
                stage[b, hr * owners + q] = window[:, :128]

        def send(j, _):
            hr = j // owners
            q = (idx + j) % owners
            copy_to(
                stage.at[b, hr * owners + q], arrived.at[b, hr * owners + idx],
                out_send.at[b], out_recv.at[b],
                {"cell": (zh + hr - 2 * zh * hr) * NY + y, "idx": q},
            ).start()
            return 0

        lax.fori_loop(1, 2 * owners, send, 0)
        arrived[b, idx] = stage[b, idx]

    def all_but_one(ref, b):
        return ref.at[b, pl.ds(0, 2 * owners - 1)]

    y_own(0, 0)
    y_own(0, 1)

    @on_source
    def _():
        z_copy_j(1).start()
        spread(0, 0)

    @on_other
    def _():
        z_copy_j(3).start()

    z_copy_t(0).start()
    z_copy_t(1).start()

    pass_on(0, 0)
    got_slab(3, 0, 0)
    got_slab(1, 0, 1)
    y_onward(0)
    start_group(0, 1)
    end_group(0, 0)
    start_group(1, 1)
    on_source(z_onward_x(1).start)
    for kk in range(2):
        got_passing(kk)
        z_onward_t(kk).start()
    on_source(z_onward_x(0).start)

    pass_on(0, 1)
    have_group(0, 0)
    got_slab(3, 0, 1)
    got_slab(1, 0, 0)
    unit(((0, 0), (1, 0), (3, 0)), 0, (0,))
    got_slab(0, 1, 0)
    y_copy(0, 1, 0, True).start()
    start_group(1, 0)
    end_group(0, 1)
    pass_on(1, 1)
    got_slab(0, 1, 1)
    y_copy(0, 1, 1, False).start()
    y_copy(0, 1, 1, True).start()
    y_copy(0, 1, 0, False).start()
    pl.semaphore_wait(ready, 3)
    signal(pair_ready, device(other_core=1))
    have_group(0, 1)
    unit(((0, 0), (1, 0), (3, 0)), 0, (1,))
    end_group(1, 1)
    got_slab(2, 0, 0)
    got_slab(2, 0, 1)
    unit(((2, 0), (0, 1)), 0, (0, 1))
    got_slab(3, 1, 0)
    got_slab(1, 1, 1)
    y_onward(1)
    pass_on(1, 0)
    on_other(got_xi)
    have_group(1, 1)
    unit(((0, 0), (0, 1), (1, 0), (3, 0), (2, 0)), 1, (1,))
    end_group(1, 0)
    got_slab(3, 1, 1)
    got_slab(1, 1, 0)
    unit(((1, 1), (3, 1)), 0, (0, 1))
    have_group(1, 0)
    unit(((0, 0), (0, 1), (1, 0), (3, 0), (2, 0)), 1, (0,))
    unit(((1, 1), (3, 1)), 1, (0, 1))
    pl.semaphore_wait(pair_ready, 1)
    send_out(0)
    got_slab(2, 1, 0)
    got_slab(2, 1, 1)
    unit(((2, 1),), 0, (0, 1))
    unit(((2, 1),), 1, (0, 1))
    send_out(1)

    for b in range(2):
        pltpu.make_async_copy(all_but_one(arrived, b), all_but_one(arrived, b), out_recv.at[b]).wait()
        same = jnp.sum(arrived[b, :owners], axis=0)
        crossed = jnp.sum(arrived[b, owners:], axis=0)
        for r in range(4):
            dy = [d for d, place in ROW_OF_DY.items() if place == b * 2 + r // 2][0]
            eh = r % 2
            k = (flip(zh, eh) * NY + (y + dy) % NY) * 2
            for kk in range(2):
                a = r * 2 + kk
                c = (r ^ 1) * 2 + kk
                o_ref[pl.ds(k + kk, 1), :] = (same[a : a + 1] + crossed[c : c + 1])[:, :own]

    for kk in range(2):
        for eh in range(2):
            y_copy(0, eh, kk, True).wait_send()
            y_copy(0, eh, kk, False).wait_send()
        y_copy(3, kk, 0, True).wait_send()
        y_copy(1, kk, 1, False).wait_send()
        z_copy_t(kk).wait_send()
        z_onward_t(kk).wait_send()
    z_copy_j(1).wait_send()

    @on_source
    def _():
        for hr in range(2):
            z_onward_x(hr).wait_send()
            for el in range(2):
                for dx in (1, 3):
                    x_copy(hr, el, dx).wait_send()
                    x_onward(hr, el, dx).wait_send()
                for dx in range(NX):
                    pair_copy(hr, el, dx).wait_send()

    for b in range(2):
        pltpu.make_async_copy(all_but_one(stage, b), all_but_one(stage, b), out_send.at[b]).wait()


def shards(coeffs, tensor):
    cells, width = coeffs.shape
    outputs, inner, full = tensor.shape
    owners = lax.axis_size("idx")
    return pl.pallas_call(
        kernel,
        out_shape=jax.ShapeDtypeStruct((16, cells // owners), F32),
        in_specs=[pl.BlockSpec(memory_space=pltpu.HBM)] * 2,
        out_specs=pl.BlockSpec(memory_space=pltpu.VMEM),
        scratch_shapes=[
            pltpu.VMEM((cells, width), BF16),
            pltpu.VMEM((2, inner, 2 * NX * width), BF16),
            pltpu.VMEM((2, inner, 2 * NX * width), BF16),
            pltpu.VMEM((16, inner, 2 * NX * width), BF16),
            pltpu.VMEM((2, width, cells), BF16),
            pltpu.VMEM((2, 2 * NX * width, cells), BF16),
            pltpu.VMEM((2, 16, cells), F32),
            pltpu.VMEM((2, 2 * owners, 8, 128), F32),
            pltpu.VMEM((2, 2 * owners, 8, 128), F32),
            pltpu.SemaphoreType.DMA,
            pltpu.SemaphoreType.DMA((4,)),
            pltpu.SemaphoreType.DMA((12,)),
            pltpu.SemaphoreType.DMA((7,)),
            pltpu.SemaphoreType.DMA((16,)),
            pltpu.SemaphoreType.DMA((16,)),
            pltpu.SemaphoreType.DMA((2,)),
            pltpu.SemaphoreType.DMA((16,)),
            pltpu.SemaphoreType.DMA((2,)),
            pltpu.SemaphoreType.DMA,
            pltpu.SemaphoreType.DMA((16,)),
            pltpu.SemaphoreType.DMA((2,)),
            pltpu.SemaphoreType.REGULAR,
            pltpu.SemaphoreType.REGULAR,
        ],
        compiler_params=pltpu.CompilerParams(
            collective_id=0, has_side_effects=True, vmem_limit_bytes=66200 * 1000
        ),
    )(coeffs, tensor.reshape(outputs * inner, full))


def solution(mesh):
    return jax.shard_map(
        shards,
        mesh=mesh,
        in_specs=(P("cell", "idx"), P("cell", "idx", None)),
        out_specs=P(None, ("cell", "idx")),
        check_vma=False,
    )
```

time: 78.5 us -> 58.6 us (0.75)
  Pallas kernels: 75.5 us -> 57.2 us
  local copies, waits for them, and re-layouts: 2.82 us -> 1.3 us
    pallas_call x1, Pallas kernels: 75.5 us -> 57.2 us  [shards(): pl.pallas_call(kernel, out_shape=jax.ShapeDtypeStruct((16, cells // owner...]
    unnamed x5 -> x1, local copies, waits for them, and re-layouts: 2.82 us -> 1.3 us
where the time goes in v2:
time: 58.6 us; the launch traced here: 58.5 us
  Pallas kernels  57.2 us (98%)
  local copies, waits for them, and re-layouts  1.3 us (2%)
    pallas_call x1, Pallas kernels, shards(): pl.pallas_call(kernel, out_shape=jax.ShapeDtypeStruct((16, cells // owner...  57.2 us
    unnamed x1, local copies, waits for them, and re-layouts  1.3 us

profile of v2, /device:TPU:1, one launch (start us, length us, event | category | flops | bytes accessed | tf_op | source)
XLA Modules:
  0.0 58.5 jit_solution(4836233902360692523)
XLA Ops:
  0.0 57.2 %shard_map.28 = f32[16,96]{1,0:T(8,128)} custom-call(bf16[1536,128]{1,0:T(8,128)(2,1)} %x_hbm.1, bf16[256,2048]{1,0:T(8,128)(2,1)} %bitcast.1), custom_call_target="tpu_custom_call" | custom-call | tf_op jit(solution)/shard_map/pallas_call | solution.py:390
  57.2 1.3 %copy.4 = f32[16,96]{1,0:T(8,128)} copy(f32[16,96]{1,0:T(8,128)} %shard_map.28) | data formatting | bytes 12288

commit v3 on v2

--- a/solution.py
+++ b/solution.py
@@ -141,7 +141,7 @@
         return block_of(hr, el, 0) if el else xi.at[hr]
 
     def x_copy(hr, el, dx):
-        n = number(hr, el, 0 if dx == 1 else 1)
+        n = number(hr, el, {1: 0, 3: 1, 2: 2}[dx])
         there = NX - dx
         return copy_to(
             first_of(hr, el), block_of(hr, el, there),
@@ -180,10 +180,6 @@
     def y_own(eh, kk):
         y_copy(0, eh, kk, True).start()
         y_copy(0, eh, 1 - kk, False).start()
-
-    def y_onward(eh):
-        y_copy(3, eh, 0, True).start()
-        y_copy(1, eh, 1, False).start()
 
     def spread(hr, el):
         x_copy(hr, el, 1).start()
@@ -246,8 +242,8 @@
         lax.fori_loop(0, cells // 256, tile, 0, unroll=True)
         begun.update((dy, eh, hr) for dy, eh in pieces)
 
-    def send_out(b):
-        for hr in range(2):
+    def send_out(b, hrs=(1, 0)):
+        for hr in hrs:
             rows = outp[hr, b * 8 : b * 8 + 8, :]
             for q in range(owners):
                 first = q * own // 128 * 128
@@ -257,18 +253,16 @@
                     window = pltpu.roll(window, window.shape[1] - shift, 1)
                 stage[b, hr * owners + q] = window[:, :128]
 
-        def send(j, _):
-            hr = j // owners
-            q = (idx + j) % owners
-            copy_to(
-                stage.at[b, hr * owners + q], arrived.at[b, hr * owners + idx],
-                out_send.at[b], out_recv.at[b],
-                {"cell": (zh + hr - 2 * zh * hr) * NY + y, "idx": q},
-            ).start()
-            return 0
-
-        lax.fori_loop(1, 2 * owners, send, 0)
-        arrived[b, idx] = stage[b, idx]
+            for j in range(1 - hr, owners):
+                q = (idx + j) % owners
+                copy_to(
+                    stage.at[b, hr * owners + q], arrived.at[b, hr * owners + idx],
+                    out_send.at[b], out_recv.at[b],
+                    {"cell": flip(zh, hr) * NY + y, "idx": q},
+                ).start()
+
+        if 0 in hrs:
+            arrived[b, idx] = stage[b, idx]
 
     def all_but_one(ref, b):
         return ref.at[b, pl.ds(0, 2 * owners - 1)]
@@ -281,17 +275,15 @@
         z_copy_j(1).start()
         spread(0, 0)
 
-    @on_other
-    def _():
-        z_copy_j(3).start()
-
     z_copy_t(0).start()
     z_copy_t(1).start()
+    on_other(z_copy_j(3).start)
 
     pass_on(0, 0)
     got_slab(3, 0, 0)
     got_slab(1, 0, 1)
-    y_onward(0)
+    y_copy(3, 0, 0, True).start()
+    y_copy(1, 0, 1, False).start()
     start_group(0, 1)
     end_group(0, 0)
     start_group(1, 1)
@@ -309,41 +301,44 @@
     got_slab(0, 1, 0)
     y_copy(0, 1, 0, True).start()
     start_group(1, 0)
-    end_group(0, 1)
     pass_on(1, 1)
     got_slab(0, 1, 1)
     y_copy(0, 1, 1, False).start()
     y_copy(0, 1, 1, True).start()
     y_copy(0, 1, 0, False).start()
+    end_group(0, 1)
     pl.semaphore_wait(ready, 3)
     signal(pair_ready, device(other_core=1))
+    unit(((0, 1),), 0, (0,))
     have_group(0, 1)
-    unit(((0, 0), (1, 0), (3, 0)), 0, (1,))
-    end_group(1, 1)
+    unit(((0, 0), (1, 0), (3, 0), (0, 1)), 0, (1,))
+    got_slab(3, 1, 0)
+    y_copy(3, 1, 0, True).start()
+    pass_on(1, 0)
+    got_slab(1, 1, 1)
+    y_copy(1, 1, 1, False).start()
     got_slab(2, 0, 0)
     got_slab(2, 0, 1)
-    unit(((2, 0), (0, 1)), 0, (0, 1))
-    got_slab(3, 1, 0)
-    got_slab(1, 1, 1)
-    y_onward(1)
-    pass_on(1, 0)
+    unit(((2, 0),), 0, (0, 1))
+    end_group(1, 1)
+    have_group(1, 1)
     on_other(got_xi)
-    have_group(1, 1)
     unit(((0, 0), (0, 1), (1, 0), (3, 0), (2, 0)), 1, (1,))
     end_group(1, 0)
     got_slab(3, 1, 1)
     got_slab(1, 1, 0)
     unit(((1, 1), (3, 1)), 0, (0, 1))
+    unit(((1, 1), (3, 1)), 1, (1,))
     have_group(1, 0)
-    unit(((0, 0), (0, 1), (1, 0), (3, 0), (2, 0)), 1, (0,))
-    unit(((1, 1), (3, 1)), 1, (0, 1))
+    unit(((0, 0), (0, 1), (1, 0), (3, 0), (2, 0), (1, 1), (3, 1)), 1, (0,))
     pl.semaphore_wait(pair_ready, 1)
     send_out(0)
     got_slab(2, 1, 0)
     got_slab(2, 1, 1)
+    unit(((2, 1),), 1, (0, 1))
+    send_out(1, (1,))
     unit(((2, 1),), 0, (0, 1))
-    unit(((2, 1),), 1, (0, 1))
-    send_out(1)
+    send_out(1, (0,))
 
     for b in range(2):
         pltpu.make_async_copy(all_but_one(arrived, b), all_but_one(arrived, b), out_recv.at[b]).wait()
@@ -418,9 +413,12 @@
             pltpu.SemaphoreType.REGULAR,
         ],
         compiler_params=pltpu.CompilerParams(
-            collective_id=0, has_side_effects=True, vmem_limit_bytes=66200 * 1000
+            collective_id=0, has_side_effects=True, vmem_limit_bytes=40 * 1024 * 1024
         ),
-    )(coeffs, tensor.reshape(outputs * inner, full))
+    )(
+        pltpu.with_memory_space_constraint(coeffs, pltpu.HBM),
+        pltpu.with_memory_space_constraint(tensor.reshape(outputs * inner, full), pltpu.HBM),
+    )
 
 
 def solution(mesh):

time: 58.6 us -> 55.1 us (0.940)
  Pallas kernels: 57.2 us -> 54.3 us
  local copies, waits for them, and re-layouts: 1.3 us -> 0.6 us
    pallas_call x1, Pallas kernels: 57.2 us -> 54.3 us  [shards(): pl.pallas_call(kernel, out_shape=jax.ShapeDtypeStruct((16, cells // owner...]
    unnamed x1, local copies, waits for them, and re-layouts: 1.3 us -> 0.6 us
where the time goes in v3:
time: 55.1 us; the launch traced here: 54.9 us
  Pallas kernels  54.3 us (99%)
  local copies, waits for them, and re-layouts  0.6 us (1%)
    pallas_call x1, Pallas kernels, shards(): pl.pallas_call(kernel, out_shape=jax.ShapeDtypeStruct((16, cells // owner...  54.3 us

profile of v3, /device:TPU:1, one launch (start us, length us, event | category | flops | bytes accessed | tf_op | source)
XLA Modules:
  0.0 54.9 jit_solution(4585996473982617664)
XLA Ops:
  0.0 54.3 %shard_map.28 = f32[16,96]{1,0:T(8,128)S(1)} custom-call(bf16[1536,128]{1,0:T(8,128)(2,1)} %x_hbm.1, bf16[256,2048]{1,0:T(8,128)(2,1)} %bitcast.1), custom_call_target="tpu_custom_call" | custom-call | tf_op jit(solution)/shard_map/pallas_call | solution.py:385
  54.3 0.6 %copy.4 = f32[16,96]{1,0:T(8,128)} copy(f32[16,96]{1,0:T(8,128)S(1)} %shard_map.28) | data formatting | bytes 12288

commit v4 on v3

--- a/solution.py
+++ b/solution.py
@@ -203,6 +203,11 @@
             for dx in (1, 3):
                 got_xj(hr, el, dx)
                 x_onward(hr, el, dx).start()
+
+    def pair_on(hr, el):
+        @on_source
+        def _():
+            for dx in (1, 3):
                 pair_copy(hr, el, dx).start()
 
     def end_group(hr, el):
@@ -280,6 +285,7 @@
     on_other(z_copy_j(3).start)
 
     pass_on(0, 0)
+    pair_on(0, 0)
     got_slab(3, 0, 0)
     got_slab(1, 0, 1)
     y_copy(3, 0, 0, True).start()
@@ -294,6 +300,7 @@
     on_source(z_onward_x(0).start)
 
     pass_on(0, 1)
+    pair_on(0, 1)
     have_group(0, 0)
     got_slab(3, 0, 1)
     got_slab(1, 0, 0)
@@ -307,6 +314,7 @@
     y_copy(0, 1, 1, True).start()
     y_copy(0, 1, 0, False).start()
     end_group(0, 1)
+    pair_on(1, 1)
     pl.semaphore_wait(ready, 3)
     signal(pair_ready, device(other_core=1))
     unit(((0, 1),), 0, (0,))
@@ -321,6 +329,7 @@
     got_slab(2, 0, 1)
     unit(((2, 0),), 0, (0, 1))
     end_group(1, 1)
+    pair_on(1, 0)
     have_group(1, 1)
     on_other(got_xi)
     unit(((0, 0), (0, 1), (1, 0), (3, 0), (2, 0)), 1, (1,))
@@ -340,6 +349,30 @@
     unit(((2, 1),), 0, (0, 1))
     send_out(1, (0,))
 
+    for kk in range(2):
+        for eh in range(2):
+            y_copy(0, eh, kk, True).wait_send()
+            y_copy(0, eh, kk, False).wait_send()
+        y_copy(3, kk, 0, True).wait_send()
+        y_copy(1, kk, 1, False).wait_send()
+        z_copy_t(kk).wait_send()
+        z_onward_t(kk).wait_send()
+    z_copy_j(1).wait_send()
+
+    @on_source
+    def _():
+        for hr in range(2):
+            z_onward_x(hr).wait_send()
+            for el in range(2):
+                for dx in (1, 3):
+                    x_copy(hr, el, dx).wait_send()
+                    x_onward(hr, el, dx).wait_send()
+                for dx in range(NX):
+                    pair_copy(hr, el, dx).wait_send()
+
+    for b in range(2):
+        pltpu.make_async_copy(all_but_one(stage, b), all_but_one(stage, b), out_send.at[b]).wait()
+
     for b in range(2):
         pltpu.make_async_copy(all_but_one(arrived, b), all_but_one(arrived, b), out_recv.at[b]).wait()
         same = jnp.sum(arrived[b, :owners], axis=0)
@@ -352,30 +385,6 @@
                 a = r * 2 + kk
                 c = (r ^ 1) * 2 + kk
                 o_ref[pl.ds(k + kk, 1), :] = (same[a : a + 1] + crossed[c : c + 1])[:, :own]
-
-    for kk in range(2):
-        for eh in range(2):
-            y_copy(0, eh, kk, True).wait_send()
-            y_copy(0, eh, kk, False).wait_send()
-        y_copy(3, kk, 0, True).wait_send()
-        y_copy(1, kk, 1, False).wait_send()
-        z_copy_t(kk).wait_send()
-        z_onward_t(kk).wait_send()
-    z_copy_j(1).wait_send()
-
-    @on_source
-    def _():
-        for hr in range(2):
-            z_onward_x(hr).wait_send()
-            for el in range(2):
-                for dx in (1, 3):
-                    x_copy(hr, el, dx).wait_send()
-                    x_onward(hr, el, dx).wait_send()
-                for dx in range(NX):
-                    pair_copy(hr, el, dx).wait_send()
-
-    for b in range(2):
-        pltpu.make_async_copy(all_but_one(stage, b), all_but_one(stage, b), out_send.at[b]).wait()
 
 
 def shards(coeffs, tensor):

time: 55.1 us -> 55 us (level)
  no operation moved by 1% of the time
where the time goes in v4:
time: 55 us; the launch traced here: 54.9 us
  Pallas kernels  54.3 us (99%)
  local copies, waits for them, and re-layouts  0.6 us (1%)
    pallas_call x1, Pallas kernels, shards(): pl.pallas_call(kernel, out_shape=jax.ShapeDtypeStruct((16, cells // owner...  54.3 us

profile of v4, /device:TPU:1, one launch (start us, length us, event | category | flops | bytes accessed | tf_op | source)
XLA Modules:
  0.0 54.9 jit_solution(15470920816871983161)
XLA Ops:
  0.0 54.3 %shard_map.28 = f32[16,96]{1,0:T(8,128)S(1)} custom-call(bf16[1536,128]{1,0:T(8,128)(2,1)} %x_hbm.1, bf16[256,2048]{1,0:T(8,128)(2,1)} %bitcast.1), custom_call_target="tpu_custom_call" | custom-call | tf_op jit(solution)/shard_map/pallas_call | solution.py:394
  54.3 0.6 %copy.4 = f32[16,96]{1,0:T(8,128)} copy(f32[16,96]{1,0:T(8,128)S(1)} %shard_map.28) | data formatting | bytes 12288

commit v5 on v4

--- a/solution.py
+++ b/solution.py
@@ -20,7 +20,7 @@
     x_hbm, t_hbm, o_ref,
     xin, outbox, passing, slab, xi, xj, outp, stage, arrived,
     in_sem, t_sem, y_send, z_send, x_send, pair_send, out_send,
-    slab_recv, pass_recv, xi_recv, xj_recv, out_recv, ready, pair_ready,
+    slab_recv, pass_recv, xi_recv, xj_recv, out_recv, ready, pair_ready, half_send, half_recv,
 ):
     cell = lax.axis_index("cell")
     idx = lax.axis_index("idx")
@@ -153,7 +153,7 @@
         src = xj.at[hr, pl.ds(el * line + dx * width + part * (width // 2), width // 2)]
         return copy_to(
             src, half_of(hr, el, part), x_send.at[number(hr, el, 2 + part)],
-            xj_recv.at[number(hr, el, 2)], device(dx=NX - dx),
+            half_recv.at[(hr * 2 + el) * 2 + part], device(dx=NX - dx),
         )
 
     def pair_copy(hr, el, dx):
@@ -162,6 +162,15 @@
         return copy_to(
             src, block_of(hr, el, dx), pair_send.at[n], xj_recv.at[n], device(other_core=1)
         )
+
+    def pair_half(hr, el, part):
+        n = (hr * 2 + el) * 2 + part
+        there = half_of(hr, el, part)
+        return copy_to(there, there, half_send.at[n], half_recv.at[n], device(other_core=1))
+
+    def got_half(hr, el, part):
+        there = half_of(hr, el, part)
+        pltpu.make_async_copy(there, there, half_recv.at[(hr * 2 + el) * 2 + part]).wait()
 
     def got_slab(dy, eh, kk):
         there = slab.at[slot(dy, eh, kk)]
@@ -213,14 +222,17 @@
     def end_group(hr, el):
         @on_source
         def _():
-            got_xj(hr, el, 2)
-            pair_copy(hr, el, 2).start()
+            for part in range(2):
+                got_half(hr, el, part)
+                pair_half(hr, el, part).start()
 
     def have_group(hr, el):
         @on_other
         def _():
-            for dx in range(NX):
+            for dx in (0, 1, 3):
                 got_xj(hr, el, dx)
+            for part in range(2):
+                got_half(hr, el, part)
 
     begun = set()
 
@@ -367,8 +379,10 @@
                 for dx in (1, 3):
                     x_copy(hr, el, dx).wait_send()
                     x_onward(hr, el, dx).wait_send()
-                for dx in range(NX):
+                for dx in (0, 1, 3):
                     pair_copy(hr, el, dx).wait_send()
+                for part in range(2):
+                    pair_half(hr, el, part).wait_send()
 
     for b in range(2):
         pltpu.make_async_copy(all_but_one(stage, b), all_but_one(stage, b), out_send.at[b]).wait()
@@ -420,6 +434,8 @@
             pltpu.SemaphoreType.DMA((2,)),
             pltpu.SemaphoreType.REGULAR,
             pltpu.SemaphoreType.REGULAR,
+            pltpu.SemaphoreType.DMA((8,)),
+            pltpu.SemaphoreType.DMA((8,)),
         ],
         compiler_params=pltpu.CompilerParams(
             collective_id=0, has_side_effects=True, vmem_limit_bytes=40 * 1024 * 1024

time: 55 us -> 55.2 us (level)
  no operation moved by 1% of the time
where the time goes in v5:
time: 55.2 us; the launch traced here: 55 us
  Pallas kernels  54.4 us (99%)
  local copies, waits for them, and re-layouts  0.6 us (1%)
    pallas_call x1, Pallas kernels, shards(): pl.pallas_call(kernel, out_shape=jax.ShapeDtypeStruct((16, cells // owner...  54.4 us

profile of v5, /device:TPU:1, one launch (start us, length us, event | category | flops | bytes accessed | tf_op | source)
XLA Modules:
  0.0 55.0 jit_solution(3358124230959906840)
XLA Ops:
  0.0 54.4 %shard_map.28 = f32[16,96]{1,0:T(8,128)S(1)} custom-call(bf16[1536,128]{1,0:T(8,128)(2,1)} %x_hbm.1, bf16[256,2048]{1,0:T(8,128)(2,1)} %bitcast.1), custom_call_target="tpu_custom_call" | custom-call | tf_op jit(solution)/shard_map/pallas_call | solution.py:408
  54.4 0.6 %copy.4 = f32[16,96]{1,0:T(8,128)} copy(f32[16,96]{1,0:T(8,128)S(1)} %shard_map.28) | data formatting | bytes 12288
